TPU v7x, 32 devices: a whole 2x2x4 slice. The times are simulated.
32 devices in a mesh: grp: 2 (over x), tile: 16 (over z, y, core).
Axes of the slice: x: 2, y: 2, z: 4, core: 2. Of those that a mesh axis runs over, the one named last changes fastest.
Arguments:
- voltages: bfloat16 [2, 32, 128, 1024], P(None, ('grp', 'tile')), parts along dimension 1, may hold values from -6 to 6
Outputs:
- visibilities: float32 [2, 2, 136, 128, 128], P(None, 'grp', None, 'tile'), parts along dimension 1
There are 2 independent parts, one for each index of `grp`. A program takes and returns all parts, laid end to end along the dimension named above; each array names one. Nothing has to cross between parts.
All inputs are finite; a program needn't handle non-finite values.
Results may differ from a plain program's by a relative error of at most 0.0003.
Values may be sent and summed in bfloat16 or wider, within the bound.
A program may use at most 64 MiB of HBM per device.

v0:
```python
import jax
import jax.numpy as jnp
import numpy as np
from jax import lax
from jax.sharding import PartitionSpec as P

NBLK = 16
TIME = 1024


def passed_along(block, axis, distance):
    devices = range(lax.axis_size(axis))
    route = [((i - distance) % len(devices), i) for i in devices]
    return lax.ppermute(block, axis, route)


def pair_tile(rows_side, cols_side):
    real_part = jnp.einsum(
        "cit,cjt->cij", rows_side[0], cols_side[0], preferred_element_type=jnp.float32
    ) + jnp.einsum("cit,cjt->cij", rows_side[1], cols_side[1], preferred_element_type=jnp.float32)
    imag_part = jnp.einsum(
        "cit,cjt->cij", rows_side[1], cols_side[0], preferred_element_type=jnp.float32
    ) - jnp.einsum("cit,cjt->cij", rows_side[0], cols_side[1], preferred_element_type=jnp.float32)
    return jnp.stack([real_part, imag_part]) / TIME


def covers_all(members, blocks_count):
    reached = set()
    for first_member in members:
        for second_member in members:
            reached.add((first_member - second_member) % blocks_count)
    return len(reached) == blocks_count


def search_cover(members, first_value, target_count, blocks_count):
    if len(members) == target_count:
        if covers_all(members, blocks_count):
            return members
        return []
    for candidate in range(first_value, blocks_count):
        outcome = search_cover(members + [candidate], candidate + 1, target_count, blocks_count)
        if outcome:
            return outcome
    return []


def cover_offsets(blocks_count):
    target_count = 2
    while target_count <= blocks_count:
        outcome = search_cover([0], 1, target_count, blocks_count)
        if outcome:
            return outcome
        target_count = target_count + 1
    return list(range(blocks_count))


def class_pair(members, distance, blocks_count):
    for first_member in members:
        for second_member in members:
            if (second_member - first_member) % blocks_count == distance:
                return (first_member, second_member)
    return (0, distance)


def cover_sources(stride, members):
    sources = []
    for row_block in range(NBLK):
        for col_block in range(row_block, NBLK):
            if row_block == col_block:
                sources.append(row_block * stride)
            else:
                gap_size = col_block - row_block
                distance = min(gap_size, NBLK - gap_size)
                first_member, second_member = class_pair(members, distance, NBLK)
                if gap_size == distance:
                    owner_block = (row_block - first_member) % NBLK
                else:
                    owner_block = (col_block - first_member) % NBLK
                sources.append(owner_block * stride + distance)
    return np.array(sources, np.int32)


def channel_order(received, slot_count, sources):
    rows_part = received.shape[4]
    width = received.shape[5]
    all_channels = received.shape[1] * received.shape[2] // NBLK
    arranged = received.reshape(2, NBLK, all_channels, slot_count, rows_part, width)
    arranged = jnp.transpose(arranged, (0, 2, 1, 3, 4, 5)).reshape(
        2, all_channels, NBLK * slot_count, rows_part, width
    )
    return jnp.take(arranged, jnp.asarray(sources), axis=2)


def on_device(voltages):
    split_count = lax.axis_size("tile") // NBLK
    own_block = lax.axis_index("tile") // split_count
    diagonal = pair_tile(voltages, voltages)
    members = cover_offsets(NBLK)
    fetched = {0: voltages}
    for member_offset in members[1:]:
        fetched[member_offset] = passed_along(voltages, "tile", -member_offset * split_count)
    tiles_list = [diagonal]
    for distance in range(1, NBLK // 2 + 1):
        first_member, second_member = class_pair(members, distance, NBLK)
        product = pair_tile(fetched[first_member], fetched[second_member])
        flipped = jnp.stack([jnp.swapaxes(product[0], 1, 2), -jnp.swapaxes(product[1], 1, 2)])
        first_block = (own_block + first_member) % NBLK
        second_block = (own_block + second_member) % NBLK
        tiles_list.append(jnp.where(first_block < second_block, product, flipped))
    tile_slots = jnp.stack(tiles_list, axis=2)
    received = lax.all_to_all(tile_slots[:, None], "tile", split_axis=4, concat_axis=1, tiled=True)
    return channel_order(received, NBLK // 2 + 1, cover_sources(NBLK // 2 + 1, members))


def solution(mesh):
    placed = (P(None, ("grp", "tile"), None, None),)
    return jax.shard_map(
        on_device,
        mesh=mesh,
        in_specs=placed,
        out_specs=P(None, "grp", None, "tile", None),
        check_vma=False,
    )
```

profile of v0, /device:TPU:1, one launch (start us, length us, event | category | flops | bytes accessed | tf_op | source)
XLA Modules:
  0.0 122.9 jit_solution(4143550448847985932)
XLA Ops:
  0.0 0.0 collective-permute-start
  0.0 5.8 %collective-permute-start.1 = (bf16[2,1,128,1024]{3,2,1,0:T(8,128)(2,1)}, bf16[2,1,128,1024]{3,2,1,0:T(8,128)(2,1)S(1)}, u32[]{:S(2)}, u32[]{:S(2)}) collective-permute-start(bf16[2,1,128,1024]{3,2,1,0:T(8,128)(2,1)} %param.2), channel_id=1, source_target_pairs={{2,0},{3,1},{4,2},{5,3},{6,4},{7,5},{8,6},{9,7},{10,8},{11,9},{12,... | collective-permute-start | bytes 1572872 | tf_op jit(solution)/shard_map/ppermute | solution.py:14
  5.8 0.4 collective-permute-start.2
  6.2 0.0 collective-permute-start.3
  6.2 1.3 %fusion.32 = f32[128,128]{1,0:T(8,128)S(1)} fusion(bf16[2,1,128,1024]{3,2,1,0:T(8,128)(2,1)} %param.2), kind=kOutput, calls=%fused_computation.60 | convolution fusion | flops 33554432 | bytes 327680 | tf_op jit(solution)/shard_map/cit,cjt->cij/dot_general | solution.py:18
  7.4 1.3 %fusion.1 = f32[1,1,1,128,128]{4,3,2,1,0:T(8,128)S(1)} fusion(f32[128,128]{1,0:T(8,128)S(1)} %fusion.32, bf16[2,1,128,1024]{3,2,1,0:T(8,128)(2,1)} %param.2), kind=kOutput, calls=%fused_computation.21 | convolution fusion | flops 33570816 | bytes 393216 | tf_op jit(solution)/shard_map/cit,cjt->cij/dot_general | solution.py:20
  8.8 1.3 %fusion.15 = f32[128,128]{1,0:T(8,128)S(1)} fusion(bf16[2,1,128,1024]{3,2,1,0:T(8,128)(2,1)} %param.2), kind=kOutput, calls=%fused_computation.43 | convolution fusion | flops 33554432 | bytes 589824 | tf_op jit(solution)/shard_map/cit,cjt->cij/dot_general | solution.py:21
  10.0 0.0 copy-done.1
  10.1 0.2 fusion
  10.3 9.7 %collective-permute-done = bf16[2,1,128,1024]{3,2,1,0:T(8,128)(2,1)S(1)} collective-permute-done((bf16[2,1,128,1024]{3,2,1,0:T(8,128)(2,1)}, bf16[2,1,128,1024]{3,2,1,0:T(8,128)(2,1)S(1)}, u32[]{:S(2)}, u32[]{:S(2)}) %collective-permute-start) | collective-permute-done | bytes 524320 | tf_op jit(solution)/shard_map/ppermute | solution.py:14
  20.0 0.2 fusion.12
  20.2 0.2 convolution_add_fusion.7
  20.5 0.2 fusion.27
  20.7 0.2 convolution_subtract_fusion.7
  20.9 0.1 copy.143
  21.0 0.0 collective-permute-done.1
  21.1 0.0 copy-start.3
  21.1 0.2 fusion.9
  21.3 0.2 fusion.24
  21.5 0.2 convolution_add_fusion.6
  21.8 0.2 convolution_subtract_fusion.6
  22.0 0.1 copy.148
  22.2 6.9 %collective-permute-done.2 = bf16[2,1,128,1024]{3,2,1,0:T(8,128)(2,1)} collective-permute-done((bf16[2,1,128,1024]{3,2,1,0:T(8,128)(2,1)}, bf16[2,1,128,1024]{3,2,1,0:T(8,128)(2,1)}, u32[]{:S(2)}, u32[]{:S(2)}) %collective-permute-start.2) | collective-permute-done | bytes 524320 | tf_op jit(solution)/shard_map/ppermute | solution.py:14
  29.1 1.2 fusion.52
  30.3 1.2 fusion.50
  31.5 1.2 convolution_add_fusion.5
  32.7 0.0 copy-done.3
  32.7 1.2 convolution_subtract_fusion.5
  33.9 0.1 copy.153
  34.0 1.2 fusion.48
  35.2 1.2 fusion.46
  36.4 1.2 convolution_add_fusion.4
  37.6 1.2 convolution_subtract_fusion.4
  38.8 0.1 copy.158
  38.9 1.2 fusion.6
  40.1 1.2 fusion.21
  41.3 1.2 convolution_add_fusion.3
  42.5 1.2 convolution_subtract_fusion.3
  43.7 0.1 copy.163
  43.8 0.0 copy-start.4
  43.9 13.2 %collective-permute-done.3 = bf16[2,1,128,1024]{3,2,1,0:T(8,128)(2,1)} collective-permute-done((bf16[2,1,128,1024]{3,2,1,0:T(8,128)(2,1)}, bf16[2,1,128,1024]{3,2,1,0:T(8,128)(2,1)}, u32[]{:S(2)}, u32[]{:S(2)}) %collective-permute-start.3) | collective-permute-done | bytes 524320 | tf_op jit(solution)/shard_map/ppermute | solution.py:14
  57.0 1.3 %fusion.51 = f32[128,128]{0,1:T(8,128)S(1)} fusion(bf16[2,1,128,1024]{3,2,1,0:T(8,128)(2,1)} %copy-done.3, bf16[2,1,128,1024]{3,2,1,0:T(8,128)(2,1)} %collective-permute-done.3), kind=kOutput, calls=%fused_computation.102 | convolution fusion | flops 33554432 | bytes 589824 | tf_op jit(solution)/shard_map/cit,cjt->cij/dot_general | solution.py:20
  58.3 1.2 fusion.49
  59.5 1.2 convolution_add_fusion.2
  60.7 1.2 convolution_subtract_fusion.2
  61.9 0.1 copy.168
  62.1 1.2 fusion.47
  63.2 1.2 fusion.45
  64.4 1.2 convolution_add_fusion.1
  65.6 1.2 convolution_subtract_fusion.1
  66.8 0.1 copy.169
  66.9 0.0 copy-start.2
  67.0 1.3 %fusion.3 = f32[128,128]{1,0:T(8,128)S(1)} fusion(bf16[2,1,128,1024]{3,2,1,0:T(8,128)(2,1)} %collective-permute-done.3, bf16[2,1,128,1024]{3,2,1,0:T(8,128)(2,1)} %param.2), kind=kOutput, calls=%fused_computation.31 | convolution fusion | flops 33554432 | bytes 589824 | tf_op jit(solution)/shard_map/cit,cjt->cij/dot_general | solution.py:20
  68.3 1.2 fusion.18
  69.5 1.2 convolution_add_fusion
  70.7 1.2 convolution_subtract_fusion
  71.9 0.1 copy.170
  72.2 2.0 %copy.171 = f32[2,1,1,9,128,128]{5,0,3,2,1,4:T(2,128)} copy(f32[2,1,1,9,128,128]{5,4,3,0,2,1:T(8,128)S(1)} %bitcast.255) | data formatting | bytes 2359296 | tf_op jit(solution)/shard_map/broadcast_in_dim | solution.py:111
  74.2 21.2 %all-to-all-start = ((f32[2,1,1,9,128,128]{5,0,3,2,1,4:T(2,128)}), f32[2,1,1,9,128,128]{5,0,3,2,1,4:T(2,128)S(1)}, u32[]{:S(2)}, u32[]{:S(2)}) async-start(f32[2,1,1,9,128,128]{5,0,3,2,1,4:T(2,128)} %copy.171), calls=%async_computation | async-start | bytes 2359296 | tf_op jit(solution)/shard_map/all_to_all | solution.py:111
  95.4 25.5 %all-to-all-done = f32[2,1,1,9,128,128]{5,0,3,2,1,4:T(2,128)S(1)} async-done(((f32[2,1,1,9,128,128]{5,0,3,2,1,4:T(2,128)}), f32[2,1,1,9,128,128]{5,0,3,2,1,4:T(2,128)S(1)}, u32[]{:S(2)}, u32[]{:S(2)}) %all-to-all-start) | async-done | bytes 1179680 | tf_op jit(solution)/shard_map/all_to_all | solution.py:111
  121.0 0.1 copy.200
  121.1 0.1 copy.173
  121.2 0.7 gather_fusion
  121.9 1.1 copy.174
  (39 shorter events, 0.5 us)
Async XLA Ops:
  0.0 10.0 %copy-start.1 = (bf16[2,1,128,1024]{3,2,1,0:T(8,128)(2,1)S(1)}, bf16[2,1,128,1024]{3,2,1,0:T(8,128)(2,1)}, u32[]{:S(2)}) copy-start(bf16[2,1,128,1024]{3,2,1,0:T(8,128)(2,1)} %param.2) | copy-start | bytes 1572868
  0.0 20.0 %collective-permute-start = (bf16[2,1,128,1024]{3,2,1,0:T(8,128)(2,1)}, bf16[2,1,128,1024]{3,2,1,0:T(8,128)(2,1)S(1)}, u32[]{:S(2)}, u32[]{:S(2)}) collective-permute-start(bf16[2,1,128,1024]{3,2,1,0:T(8,128)(2,1)} %param.2), channel_id=1, source_target_pairs={{1,0},{2,1},{3,2},{4,3},{5,4},{6,5},{7,6},{8,7},{9,8},{10,9},{11,1... | collective-permute-start | bytes 1572872 | tf_op jit(solution)/shard_map/ppermute | solution.py:14
  0.0 21.0 %collective-permute-start.1 = (bf16[2,1,128,1024]{3,2,1,0:T(8,128)(2,1)}, bf16[2,1,128,1024]{3,2,1,0:T(8,128)(2,1)S(1)}, u32[]{:S(2)}, u32[]{:S(2)}) collective-permute-start(bf16[2,1,128,1024]{3,2,1,0:T(8,128)(2,1)} %param.2), channel_id=1, source_target_pairs={{2,0},{3,1},{4,2},{5,3},{6,4},{7,5},{8,6},{9,7},{10,8},{11,9},{12,... | collective-permute-start | bytes 1572872 | tf_op jit(solution)/shard_map/ppermute | solution.py:14
  5.8 23.3 %collective-permute-start.2 = (bf16[2,1,128,1024]{3,2,1,0:T(8,128)(2,1)}, bf16[2,1,128,1024]{3,2,1,0:T(8,128)(2,1)}, u32[]{:S(2)}, u32[]{:S(2)}) collective-permute-start(bf16[2,1,128,1024]{3,2,1,0:T(8,128)(2,1)} %param.2), channel_id=1, source_target_pairs={{5,0},{6,1},{7,2},{8,3},{9,4},{10,5},{11,6},{12,7},{13,8},{14,9},{... | collective-permute-start | bytes 1572872 | tf_op jit(solution)/shard_map/ppermute | solution.py:14
  6.2 50.9 %collective-permute-start.3 = (bf16[2,1,128,1024]{3,2,1,0:T(8,128)(2,1)}, bf16[2,1,128,1024]{3,2,1,0:T(8,128)(2,1)}, u32[]{:S(2)}, u32[]{:S(2)}) collective-permute-start(bf16[2,1,128,1024]{3,2,1,0:T(8,128)(2,1)} %param.2), channel_id=1, source_target_pairs={{8,0},{9,1},{10,2},{11,3},{12,4},{13,5},{14,6},{15,7},{0,8},{1,9},... | collective-permute-start | bytes 1572872 | tf_op jit(solution)/shard_map/ppermute | solution.py:14
  21.1 11.6 %copy-start.3 = (bf16[2,1,128,1024]{3,2,1,0:T(8,128)(2,1)}, bf16[2,1,128,1024]{3,2,1,0:T(8,128)(2,1)S(1)}, u32[]{:S(2)}) copy-start(bf16[2,1,128,1024]{3,2,1,0:T(8,128)(2,1)S(1)} %collective-permute-done.1) | copy-start | bytes 1572868
  43.8 14.5 %copy-start.4 = (bf16[2,1,128,1024]{3,2,1,0:T(8,128)(2,1)S(1)}, bf16[2,1,128,1024]{3,2,1,0:T(8,128)(2,1)}, u32[]{:S(2)}) copy-start(bf16[2,1,128,1024]{3,2,1,0:T(8,128)(2,1)} %copy-done.3) | copy-start | bytes 1572868
  66.9 1.4 %copy-start.2 = (bf16[2,1,128,1024]{3,2,1,0:T(8,128)(2,1)S(1)}, bf16[2,1,128,1024]{3,2,1,0:T(8,128)(2,1)}, u32[]{:S(2)}) copy-start(bf16[2,1,128,1024]{3,2,1,0:T(8,128)(2,1)} %param.2) | copy-start | bytes 1572868
  74.2 21.2 %copy-start = (s32[136]{0:T(256)S(1)}, s32[136]{0:T(256)}, u32[]{:S(2)}) copy-start(s32[136]{0:T(256)} %constant.111) | copy-start | bytes 1636
  74.2 46.7 %all-to-all-start = ((f32[2,1,1,9,128,128]{5,0,3,2,1,4:T(2,128)}), f32[2,1,1,9,128,128]{5,0,3,2,1,4:T(2,128)S(1)}, u32[]{:S(2)}, u32[]{:S(2)}) async-start(f32[2,1,1,9,128,128]{5,0,3,2,1,4:T(2,128)} %copy.171), calls=%async_computation | async-start | bytes 2359296 | tf_op jit(solution)/shard_map/all_to_all | solution.py:111
where the time goes:
time: 125 us; the launch traced here: 123 us
  waiting for transfers between devices  55.3 us (44%)
  matrix products  34.4 us (28%)
  starting transfers between devices  27.3 us (22%)
  local copies, waits for them, and re-layouts  4.72 us (4%)
    ppermute x4, waiting for transfers between devices, passed_along(): return lax.ppermute(block, axis, route)  29.7 us
    all_to_all x1, waiting for transfers between devices, on_device(): lax.all_to_all(tile_slots[:, None], 'tile', split_axis=4, concat_axis=1,...  25.5 us
    all_to_all x1, starting transfers between devices, on_device(): lax.all_to_all(tile_slots[:, None], 'tile', split_axis=4, concat_axis=1,...  21.2 us
    dot_general x9, matrix products, pair_tile(): jnp.einsum('cit,cjt->cij', rows_side[1], cols_side[1], preferred_element_...  9 us
    dot_general x9, matrix products, pair_tile(): jnp.einsum('cit,cjt->cij', rows_side[0], cols_side[0], preferred_element_...  8.85 us
    dot_general x9, matrix products, pair_tile(): jnp.einsum('cit,cjt->cij', rows_side[1], cols_side[0], preferred_element_...  8.8 us
    dot_general x9, matrix products, pair_tile(): jnp.einsum('cit,cjt->cij', rows_side[0], cols_side[1], preferred_element_...  7.77 us
    ppermute x4, starting transfers between devices, passed_along(): return lax.ppermute(block, axis, route)  6.16 us
  transfers between devices with their start and end apart: 5, of which 4 were waited for; matrix products, arithmetic and copies ran while one was open for 17% of the time, Pallas kernels for 0%

commit v1 on v0

--- a/solution.py
+++ b/solution.py
@@ -2,6 +2,8 @@
 import jax.numpy as jnp
 import numpy as np
 from jax import lax
+from jax.experimental import pallas as pl
+from jax.experimental.pallas import tpu as pltpu
 from jax.sharding import PartitionSpec as P
 
 NBLK = 16
@@ -112,10 +114,238 @@
     return channel_order(received, NBLK // 2 + 1, cover_sources(NBLK // 2 + 1, members))
 
 
+CORES = 2
+ROWS = 2
+LEFT, RIGHT, ACROSS, SIBLING = range(4)
+
+
+def item_edges(depth, home, half):
+    edges = []
+    detour = half == 1 and home in (0, depth - 1)
+    for row in range(ROWS):
+        if row == 0 or detour:
+            edges += [(z, row, LEFT) for z in range(home, 0, -1)]
+            edges += [(z, row, RIGHT) for z in range(home, depth - 1)]
+    crossings = [home] if detour else range(depth)
+    edges += [(z, 0, ACROSS) for z in crossings]
+    return edges
+
+
+def landing(edge):
+    z, row, way = edge
+    return {LEFT: (z - 1, row), RIGHT: (z + 1, row), ACROSS: (z, 1 - row)}[way]
+
+
+def arrival_plan(depth):
+    onward = {}
+    for home in range(depth):
+        for half in range(2):
+            for edge in item_edges(depth, home, half):
+                onward.setdefault((home, half, edge[0], edge[1]), []).append(edge[2])
+    link_free = {}
+    pending = []
+    order = 0
+    for half in range(2):
+        for home in range(depth):
+            pending.append((0.0, order, home, half, home, 0))
+            order += 1
+    events = {z: [] for z in range(depth)}
+    while pending:
+        pending.sort()
+        time, _, home, half, z, row = pending.pop(0)
+        ways = onward.get((home, half, z, row), [])
+        if (z, row) != (home, 0):
+            events[z].append((time, home, row, half, tuple(ways)))
+        for way in ways:
+            for mirrored in (0, 1):
+                link_free.setdefault((z, way), 0.0)
+            begin = max(time, link_free[(z, way)])
+            link_free[(z, way)] = begin + 1.0
+            nz, nrow = landing((z, row, way))
+            pending.append((begin + 1.1, order, home, half, nz, nrow))
+            order += 1
+    return {z: sorted(found) for z, found in events.items()}
+
+
+def tile_number(row_block, col_block):
+    return row_block * NBLK - row_block * (row_block - 1) // 2 + col_block - row_block
+
+
+def correlate_kernel(depth, x_ref, out_ref, held, row_scratch, lhs, local_sem, send_sem, recv_sem):
+    me = lax.axis_index("tile")
+    z = me // (ROWS * CORES)
+    row = (me // CORES) % ROWS
+    core = me % CORES
+    rows_part = out_ref.shape[3]
+
+    def index_of(z_of, row_of, core_of):
+        return (z_of * ROWS + row_of) * CORES + core_of
+
+    def neighbour(way):
+        return {
+            LEFT: me - ROWS * CORES,
+            RIGHT: me + ROWS * CORES,
+            ACROSS: index_of(z, 1 - row, core),
+            SIBLING: index_of(z, row, 1 - core),
+        }[way]
+
+    def greet(way):
+        pl.semaphore_signal(
+            pltpu.get_barrier_semaphore(),
+            inc=1,
+            device_id={"tile": neighbour(way)},
+            device_id_type=pl.DeviceIdType.MESH,
+        )
+
+    def transfer(block, half, way):
+        return pltpu.make_async_remote_copy(
+            src_ref=held.at[half, block],
+            dst_ref=held.at[half, block],
+            send_sem=send_sem.at[way, block, half],
+            recv_sem=recv_sem.at[block, half],
+            device_id={"tile": neighbour(way)},
+            device_id_type=pl.DeviceIdType.MESH,
+        )
+
+    def own_copy(half):
+        return pltpu.make_async_copy(x_ref.at[half, 0], held.at[half, me], local_sem.at[half])
+
+    for half in range(2):
+        own_copy(half).start()
+    greet(ACROSS)
+    greet(SIBLING)
+
+    @pl.when(z > 0)
+    def _():
+        greet(LEFT)
+
+    @pl.when(z < depth - 1)
+    def _():
+        greet(RIGHT)
+
+    barrier = pltpu.get_barrier_semaphore()
+    inner = jnp.logical_and(z > 0, z < depth - 1)
+
+    @pl.when(inner)
+    def _():
+        pl.semaphore_wait(barrier, 4)
+
+    @pl.when(jnp.logical_not(inner))
+    def _():
+        pl.semaphore_wait(barrier, 3)
+
+    for half in range(2):
+        own_copy(half).wait()
+
+        @pl.when(z > 0)
+        def _():
+            transfer(me, half, LEFT).start()
+
+        @pl.when(z < depth - 1)
+        def _():
+            transfer(me, half, RIGHT).start()
+
+        transfer(me, half, ACROSS).start()
+        transfer(me, half, SIBLING).start()
+
+    plan = arrival_plan(depth)
+    for z_static in range(depth):
+
+        @pl.when(z == z_static)
+        def _():
+            for _, home, row_of, half, ways in plan[z_static]:
+                block = index_of(home, row ^ row_of, core)
+                transfer(block, half, SIBLING).wait_recv()
+                for way in ways:
+                    transfer(block, half, way).start()
+                transfer(block, half, SIBLING).start()
+
+    for other in range(NBLK // CORES):
+        for half in range(2):
+            transfer(other * CORES + 1 - core, half, SIBLING).wait_recv()
+
+    pair = me // 2
+    odd = (me % 2) == 1
+    for block in range(NBLK):
+        halves = []
+        for half in range(2):
+            both = held[half, block, pl.ds(pl.multiple_of(pair * 2 * rows_part, 2 * rows_part), 2 * rows_part), :]
+            both = both.astype(jnp.float32)
+            halves.append(jnp.where(odd, both[rows_part:], both[:rows_part]))
+        time = halves[0].shape[1]
+        stacked = jnp.concatenate(
+            [jnp.concatenate(halves, axis=1), jnp.concatenate([halves[1], -halves[0]], axis=1)], axis=0
+        )
+        lhs[2 * rows_part * block : 2 * rows_part * (block + 1), :] = stacked.astype(jnp.bfloat16)
+
+    width = held.shape[2]
+    for first in range(0, NBLK, 2):
+        used = 2 * rows_part * (first + 2)
+        total = None
+        for half in range(2):
+            columns = held[half, first : first + 2].reshape(2 * width, time)
+            product = lax.dot_general(
+                lhs[:used, half * time : (half + 1) * time],
+                columns,
+                (((1,), (1,)), ((), ())),
+                preferred_element_type=jnp.float32,
+            )
+            total = product if total is None else total + product
+        total = total * (1.0 / time)
+        for col_block in (first, first + 1):
+            shift = (col_block - first) * width
+            for row_block in range(col_block + 1):
+                for part in range(2):
+                    top = (2 * row_block + part) * rows_part
+                    out_ref[part, 0, tile_number(row_block, col_block)] = total[top : top + rows_part, shift : shift + width]
+
+    for z_static in range(depth):
+
+        @pl.when(z == z_static)
+        def _():
+            for half in range(2):
+                if z_static > 0:
+                    transfer(me, half, LEFT).wait_send()
+                if z_static < depth - 1:
+                    transfer(me, half, RIGHT).wait_send()
+                transfer(me, half, ACROSS).wait_send()
+                transfer(me, half, SIBLING).wait_send()
+            for _, home, row_of, half, ways in plan[z_static]:
+                block = index_of(home, row ^ row_of, core)
+                for way in ways:
+                    transfer(block, half, way).wait_send()
+                transfer(block, half, SIBLING).wait_send()
+
+
+def gathered(voltages):
+    parts, _, width, time = voltages.shape
+    depth = NBLK // (ROWS * CORES)
+    tiles = NBLK * (NBLK + 1) // 2
+    rows_part = width // lax.axis_size("tile")
+    return pl.pallas_call(
+        lambda *refs: correlate_kernel(depth, *refs),
+        out_shape=jax.ShapeDtypeStruct((parts, 1, tiles, rows_part, width), jnp.float32),
+        in_specs=[pl.BlockSpec(memory_space=pl.ANY)],
+        out_specs=pl.BlockSpec(memory_space=pltpu.VMEM),
+        scratch_shapes=[
+            pltpu.VMEM((parts, NBLK, width, time), voltages.dtype),
+            pltpu.VMEM((8, 128), jnp.float32),
+            pltpu.VMEM((2 * rows_part * NBLK, 2 * time), jnp.bfloat16),
+            pltpu.SemaphoreType.DMA((2,)),
+            pltpu.SemaphoreType.DMA((4, NBLK, 2)),
+            pltpu.SemaphoreType.DMA((NBLK, 2)),
+        ],
+        compiler_params=pltpu.CompilerParams(
+            collective_id=0, has_side_effects=True, vmem_limit_bytes=56 * 2**20
+        ),
+    )(voltages)
+
+
 def solution(mesh):
     placed = (P(None, ("grp", "tile"), None, None),)
+    one_block_each = mesh.shape["tile"] == NBLK
     return jax.shard_map(
-        on_device,
+        gathered if one_block_each else on_device,
         mesh=mesh,
         in_specs=placed,
         out_specs=P(None, "grp", None, "tile", None),

time: 125 us -> 53.5 us (0.43); the launches traced: 123 us -> 53.3 us
  waiting for transfers between devices: 55.3 us -> 0 us
  Pallas kernels: 0 us -> 51 us
  matrix products: 34.4 us -> 0 us
  starting transfers between devices: 27.3 us -> 0 us
  local copies, waits for them, and re-layouts: 4.72 us -> 2.31 us
    pallas_call x0 -> x1, Pallas kernels: none -> 51 us  [gathered(): pl.pallas_call(lambda *refs: correlate_kernel(depth, *refs), out_shape=ja...]
    dot_general x36 -> x0, matrix products: 34.4 us -> none  [the longest x9 9 us: pair_tile(): jnp.einsum('cit,cjt->cij', rows_side[1], cols_side[1], preferred_element_...]
    ppermute x4 -> x0, waiting for transfers between devices: 29.7 us -> none  [passed_along(): return lax.ppermute(block, axis, route)]
    all_to_all x1 -> x0, waiting for transfers between devices: 25.5 us -> none  [on_device(): lax.all_to_all(tile_slots[:, None], 'tile', split_axis=4, concat_axis=1,...]
    all_to_all x1 -> x0, starting transfers between devices: 21.2 us -> none  [on_device(): lax.all_to_all(tile_slots[:, None], 'tile', split_axis=4, concat_axis=1,...]
    ppermute x4 -> x0, starting transfers between devices: 6.16 us -> none  [passed_along(): return lax.ppermute(block, axis, route)]
    unnamed x10 -> x1, local copies, waits for them, and re-layouts: 0.03 us -> 2.31 us
    broadcast_in_dim x1 -> x0, local copies, waits for them, and re-layouts: 1.97 us -> none  [on_device(): tile_slots[:, None]]
  transfers between devices with their start and end apart: 5 -> 0, of which waited for: 4 -> 0; matrix products, arithmetic and copies ran while one was open for 17% -> 0% of each run, Pallas kernels for 0% -> 0%
where the time goes in v1:
time: 53.5 us; the launch traced here: 53.3 us
  Pallas kernels  51 us (95%)
  local copies, waits for them, and re-layouts  2.31 us (4%)
    pallas_call x1, Pallas kernels, gathered(): pl.pallas_call(lambda *refs: correlate_kernel(depth, *refs), out_shape=ja...  51 us
    unnamed x1, local copies, waits for them, and re-layouts  2.31 us

profile of v1, /device:TPU:1, one launch (start us, length us, event | category | flops | bytes accessed | tf_op | source)
XLA Modules:
  0.0 53.3 jit_solution(8925638782563064990)
XLA Ops:
  0.0 51.0 %shard_map.17 = f32[2,1,136,8,128]{4,3,2,1,0:T(8,128)} custom-call(bf16[2,1,128,1024]{3,2,1,0:T(8,128)(2,1)} %refs_0_.1), custom_call_target="tpu_custom_call" | custom-call | tf_op jit(solution)/shard_map/pallas_call | solution.py:325
  51.0 2.3 %copy.3 = f32[2,1,136,8,128]{4,3,2,1,0:T(8,128)} copy(f32[2,1,136,8,128]{4,3,2,1,0:T(8,128)} %shard_map.17) | data formatting | bytes 2228224

commit v2 on v1

--- a/solution.py
+++ b/solution.py
@@ -125,8 +125,8 @@
     for row in range(ROWS):
         if row == 0 or detour:
             edges += [(z, row, LEFT) for z in range(home, 0, -1)]
-            edges += [(z, row, RIGHT) for z in range(home, depth - 1)]
-    crossings = [home] if detour else range(depth)
+            edges += [(z, row, RIGHT) for z in range(home, depth - 1 if home else depth - 2)]
+    crossings = [home] if detour else range(depth if home else depth - 1)
     edges += [(z, 0, ACROSS) for z in crossings]
     return edges
 
@@ -167,11 +167,15 @@
     return {z: sorted(found) for z, found in events.items()}
 
 
+def is_late(depth, z, event):
+    return z == 0 and event[1] == depth - 1 and event[2] == 1
+
+
 def tile_number(row_block, col_block):
     return row_block * NBLK - row_block * (row_block - 1) // 2 + col_block - row_block
 
 
-def correlate_kernel(depth, x_ref, out_ref, held, row_scratch, lhs, local_sem, send_sem, recv_sem):
+def correlate_kernel(depth, x_ref, out_ref, held, lhs, made, given, local_sem, send_sem, recv_sem, made_sem):
     me = lax.axis_index("tile")
     z = me // (ROWS * CORES)
     row = (me // CORES) % ROWS
@@ -197,16 +201,34 @@
             device_id_type=pl.DeviceIdType.MESH,
         )
 
-    def transfer(block, half, way):
+    width = held.shape[2]
+    time = held.shape[3]
+    chip_rows = CORES * rows_part
+    last = depth - 1
+
+    def transfer(block, half, way, chip=None):
+        place = held.at[half, block]
+        if chip is not None:
+            place = place.at[pl.ds(pl.multiple_of(chip * chip_rows, chip_rows), chip_rows)]
         return pltpu.make_async_remote_copy(
-            src_ref=held.at[half, block],
-            dst_ref=held.at[half, block],
+            src_ref=place,
+            dst_ref=place,
             send_sem=send_sem.at[way, block, half],
             recv_sem=recv_sem.at[block, half],
             device_id={"tile": neighbour(way)},
             device_id_type=pl.DeviceIdType.MESH,
         )
 
+    def handover():
+        return pltpu.make_async_remote_copy(
+            src_ref=made,
+            dst_ref=given,
+            send_sem=made_sem.at[0],
+            recv_sem=made_sem.at[1],
+            device_id={"tile": neighbour(RIGHT)},
+            device_id_type=pl.DeviceIdType.MESH,
+        )
+
     def own_copy(half):
         return pltpu.make_async_copy(x_ref.at[half, 0], held.at[half, me], local_sem.at[half])
 
@@ -249,37 +271,57 @@
         transfer(me, half, SIBLING).start()
 
     plan = arrival_plan(depth)
+    chip = me // CORES
+    thin_items = [(home_row, half) for home_row in range(ROWS) for half in range(2)]
+
+    def take_in(z_static, late):
+        for event in plan[z_static]:
+            _, home, row_of, half, ways = event
+            if is_late(depth, z_static, event) != late:
+                continue
+            block = index_of(home, row ^ row_of, core)
+            transfer(block, half, SIBLING).wait_recv()
+            for way in ways:
+                transfer(block, half, way).start()
+            if home == 0 and z_static == last - 1:
+                transfer(block, half, RIGHT, chip + ROWS).start()
+            transfer(block, half, SIBLING).start()
+
+    def take_from_sibling(z_static, late):
+        for home in range(depth):
+            for row_of in range(ROWS):
+                if is_late(depth, z_static, (0, home, row_of)) != late:
+                    continue
+                block = index_of(home, row ^ row_of, 1 - core)
+                for half in range(2):
+                    thin = z_static == last and home == 0
+                    transfer(block, half, SIBLING, chip if thin else None).wait_recv()
+
     for z_static in range(depth):
 
         @pl.when(z == z_static)
         def _():
-            for _, home, row_of, half, ways in plan[z_static]:
-                block = index_of(home, row ^ row_of, core)
-                transfer(block, half, SIBLING).wait_recv()
-                for way in ways:
-                    transfer(block, half, way).start()
-                transfer(block, half, SIBLING).start()
-
-    for other in range(NBLK // CORES):
-        for half in range(2):
-            transfer(other * CORES + 1 - core, half, SIBLING).wait_recv()
-
-    pair = me // 2
-    odd = (me % 2) == 1
-    for block in range(NBLK):
+            take_in(z_static, False)
+            if z_static == last:
+                for home_row, half in thin_items:
+                    block = index_of(0, home_row, core)
+                    transfer(block, half, RIGHT, chip).wait_recv()
+                    transfer(block, half, SIBLING, chip).start()
+            take_from_sibling(z_static, False)
+
+    def set_rows(block, device):
+        odd = (device % 2) == 1
+        start = pl.multiple_of((device // CORES) * chip_rows, chip_rows)
         halves = []
         for half in range(2):
-            both = held[half, block, pl.ds(pl.multiple_of(pair * 2 * rows_part, 2 * rows_part), 2 * rows_part), :]
-            both = both.astype(jnp.float32)
+            both = held[half, block, pl.ds(start, chip_rows), :].astype(jnp.float32)
             halves.append(jnp.where(odd, both[rows_part:], both[:rows_part]))
-        time = halves[0].shape[1]
         stacked = jnp.concatenate(
             [jnp.concatenate(halves, axis=1), jnp.concatenate([halves[1], -halves[0]], axis=1)], axis=0
         )
         lhs[2 * rows_part * block : 2 * rows_part * (block + 1), :] = stacked.astype(jnp.bfloat16)
 
-    width = held.shape[2]
-    for first in range(0, NBLK, 2):
+    def pair_product(first):
         used = 2 * rows_part * (first + 2)
         total = None
         for half in range(2):
@@ -291,7 +333,9 @@
                 preferred_element_type=jnp.float32,
             )
             total = product if total is None else total + product
-        total = total * (1.0 / time)
+        return total * (1.0 / time)
+
+    def spread(first, total):
         for col_block in (first, first + 1):
             shift = (col_block - first) * width
             for row_block in range(col_block + 1):
@@ -299,6 +343,48 @@
                     top = (2 * row_block + part) * rows_part
                     out_ref[part, 0, tile_number(row_block, col_block)] = total[top : top + rows_part, shift : shift + width]
 
+    chip_blocks = ROWS * CORES
+    handed = range(0, chip_blocks, 2)
+
+    @pl.when(z == last - 1)
+    def _():
+        for block in range(chip_blocks):
+            set_rows(block, me + chip_blocks)
+        for first in handed:
+            total = pair_product(first)
+            made[first // 2, : total.shape[0], :] = total
+
+    for block in range(NBLK - chip_blocks):
+        set_rows(block, me)
+
+    @pl.when(z == last - 1)
+    def _():
+        handover().start()
+
+    @pl.when(z < last)
+    def _():
+        for first in handed:
+            spread(first, pair_product(first))
+
+    for first in range(chip_blocks, NBLK - chip_blocks, 2):
+        spread(first, pair_product(first))
+
+    @pl.when(z == 0)
+    def _():
+        take_in(0, True)
+        take_from_sibling(0, True)
+
+    for block in range(NBLK - chip_blocks, NBLK):
+        set_rows(block, me)
+    for first in range(NBLK - chip_blocks, NBLK, 2):
+        spread(first, pair_product(first))
+
+    @pl.when(z == last)
+    def _():
+        handover().wait_recv()
+        for first in handed:
+            spread(first, given[first // 2])
+
     for z_static in range(depth):
 
         @pl.when(z == z_static)
@@ -306,7 +392,7 @@
             for half in range(2):
                 if z_static > 0:
                     transfer(me, half, LEFT).wait_send()
-                if z_static < depth - 1:
+                if z_static < last:
                     transfer(me, half, RIGHT).wait_send()
                 transfer(me, half, ACROSS).wait_send()
                 transfer(me, half, SIBLING).wait_send()
@@ -314,7 +400,20 @@
                 block = index_of(home, row ^ row_of, core)
                 for way in ways:
                     transfer(block, half, way).wait_send()
+                if home == 0 and z_static == last - 1:
+                    transfer(block, half, RIGHT, chip + ROWS).wait_send()
                 transfer(block, half, SIBLING).wait_send()
+            if z_static == last - 1:
+                handover().wait_send()
+            if z_static == last:
+                for home_row, half in thin_items:
+                    transfer(index_of(0, home_row, core), half, SIBLING, chip).wait_send()
+
+
+def write_out(tiled_ref, out_ref, sem):
+    copy = pltpu.make_async_copy(tiled_ref, out_ref, sem)
+    copy.start()
+    copy.wait()
 
 
 def gathered(voltages):
@@ -322,23 +421,33 @@
     depth = NBLK // (ROWS * CORES)
     tiles = NBLK * (NBLK + 1) // 2
     rows_part = width // lax.axis_size("tile")
-    return pl.pallas_call(
+    tiled = pl.pallas_call(
         lambda *refs: correlate_kernel(depth, *refs),
         out_shape=jax.ShapeDtypeStruct((parts, 1, tiles, rows_part, width), jnp.float32),
-        in_specs=[pl.BlockSpec(memory_space=pl.ANY)],
+        in_specs=[pl.BlockSpec(memory_space=pltpu.HBM)],
         out_specs=pl.BlockSpec(memory_space=pltpu.VMEM),
         scratch_shapes=[
             pltpu.VMEM((parts, NBLK, width, time), voltages.dtype),
-            pltpu.VMEM((8, 128), jnp.float32),
             pltpu.VMEM((2 * rows_part * NBLK, 2 * time), jnp.bfloat16),
+            pltpu.VMEM((ROWS, 2 * rows_part * ROWS * CORES, 2 * width), jnp.float32),
+            pltpu.VMEM((ROWS, 2 * rows_part * ROWS * CORES, 2 * width), jnp.float32),
             pltpu.SemaphoreType.DMA((2,)),
             pltpu.SemaphoreType.DMA((4, NBLK, 2)),
             pltpu.SemaphoreType.DMA((NBLK, 2)),
+            pltpu.SemaphoreType.DMA((2,)),
         ],
         compiler_params=pltpu.CompilerParams(
-            collective_id=0, has_side_effects=True, vmem_limit_bytes=56 * 2**20
+            collective_id=0, has_side_effects=True, vmem_limit_bytes=24 * 2**20
         ),
     )(voltages)
+    return pl.pallas_call(
+        write_out,
+        out_shape=jax.ShapeDtypeStruct(tiled.shape, tiled.dtype),
+        in_specs=[pl.BlockSpec(memory_space=pltpu.VMEM)],
+        out_specs=pl.BlockSpec(memory_space=pl.ANY),
+        scratch_shapes=[pltpu.SemaphoreType.DMA],
+        compiler_params=pltpu.CompilerParams(vmem_limit_bytes=8 * 2**20),
+    )(tiled)
 
 
 def solution(mesh):

time: 53.5 us -> 50.3 us (0.940)
  Pallas kernels: 51 us -> 49.1 us
  local copies, waits for them, and re-layouts: 2.31 us -> 1.04 us
    pallas_call x1, Pallas kernels: 51 us -> 48.1 us  [gathered(): pl.pallas_call(lambda *refs: correlate_kernel(depth, *refs), out_shape=ja...]
    unnamed x1 -> x2, local copies, waits for them, and re-layouts: 2.31 us -> 1.04 us
    pallas_call x0 -> x1, Pallas kernels: none -> 1 us  [gathered(): pl.pallas_call(write_out, out_shape=jax.ShapeDtypeStruct(tiled.shape, til...]
where the time goes in v2:
time: 50.3 us; the launch traced here: 50.2 us
  Pallas kernels  49.1 us (98%)
  local copies, waits for them, and re-layouts  1.04 us (2%)
    pallas_call x1, Pallas kernels, gathered(): pl.pallas_call(lambda *refs: correlate_kernel(depth, *refs), out_shape=ja...  48.1 us
    unnamed x2, local copies, waits for them, and re-layouts  1.04 us

profile of v2, /device:TPU:1, one launch (start us, length us, event | category | flops | bytes accessed | tf_op | source)
XLA Modules:
  0.0 50.2 jit_solution(15883455639982633456)
XLA Ops:
  0.0 0.0 copy-start
  0.0 1.0 %copy-done = bf16[2,1,128,1024]{3,2,1,0:T(8,128)(2,1)S(1)} copy-done((bf16[2,1,128,1024]{3,2,1,0:T(8,128)(2,1)S(1)}, bf16[2,1,128,1024]{3,2,1,0:T(8,128)(2,1)}, u32[]{:S(2)}) %copy-start) | copy-done | bytes 524312
  1.0 48.1 %shard_map.17.tiled_ref = f32[2,1,136,8,128]{4,3,2,1,0:T(8,128)S(1)} custom-call(bf16[2,1,128,1024]{3,2,1,0:T(8,128)(2,1)S(1)} %copy-done), custom_call_target="tpu_custom_call" | custom-call | tf_op jit(solution)/shard_map/pallas_call | solution.py:424
  49.2 1.0 %shard_map.18 = f32[2,1,136,8,128]{4,3,2,1,0:T(8,128)} custom-call(f32[2,1,136,8,128]{4,3,2,1,0:T(8,128)S(1)} %shard_map.17.tiled_ref), custom_call_target="tpu_custom_call" | custom-call | tf_op jit(solution)/shard_map/pallas_call | solution.py:443
Async XLA Ops:
  0.0 1.0 %copy-start = (bf16[2,1,128,1024]{3,2,1,0:T(8,128)(2,1)S(1)}, bf16[2,1,128,1024]{3,2,1,0:T(8,128)(2,1)}, u32[]{:S(2)}) copy-start(bf16[2,1,128,1024]{3,2,1,0:T(8,128)(2,1)} %refs_0_.1) | copy-start | bytes 1572868

commit v3 on v2

--- a/solution.py
+++ b/solution.py
@@ -120,15 +120,24 @@
 
 
 def item_edges(depth, home, half):
-    edges = []
-    detour = half == 1 and home in (0, depth - 1)
-    for row in range(ROWS):
-        if row == 0 or detour:
-            edges += [(z, row, LEFT) for z in range(home, 0, -1)]
-            edges += [(z, row, RIGHT) for z in range(home, depth - 1 if home else depth - 2)]
-    crossings = [home] if detour else range(depth if home else depth - 1)
-    edges += [(z, 0, ACROSS) for z in crossings]
-    return edges
+    last = depth - 1
+    low = 1 if home == last else 0
+    high = last - 1 if home == 0 else last
+    edges = [(z, 0, LEFT) for z in range(home, low, -1)] + [(z, 0, RIGHT) for z in range(home, high)]
+    if home == 0:
+        reach = high if half == 1 else high - 1
+        edges += [(z, 1, RIGHT) for z in range(home, reach)]
+        crossings = [home] + list(range(reach + 1, high + 1))
+    elif home == last:
+        reach = low if half == 1 else low + 1
+        edges += [(z, 1, LEFT) for z in range(home, reach, -1)]
+        crossings = [home] + list(range(low, reach))
+    elif home == 1 and half == 1:
+        edges += [(last - 1, 1, RIGHT)]
+        crossings = range(last)
+    else:
+        crossings = range(depth)
+    return edges + [(z, 0, ACROSS) for z in crossings]
 
 
 def landing(edge):
@@ -168,14 +177,14 @@
 
 
 def is_late(depth, z, event):
-    return z == 0 and event[1] == depth - 1 and event[2] == 1
+    return z < 2 and event[1] == depth - 2 + z and event[2] == 1
 
 
 def tile_number(row_block, col_block):
     return row_block * NBLK - row_block * (row_block - 1) // 2 + col_block - row_block
 
 
-def correlate_kernel(depth, x_ref, out_ref, held, lhs, made, given, local_sem, send_sem, recv_sem, made_sem):
+def correlate_kernel(depth, x_ref, out_ref, held, lhs, made, given, far_made, far_given, local_sem, send_sem, recv_sem, made_sem, far_sem):
     me = lax.axis_index("tile")
     z = me // (ROWS * CORES)
     row = (me // CORES) % ROWS
@@ -229,6 +238,17 @@
             device_id_type=pl.DeviceIdType.MESH,
         )
 
+    def far_handover(part):
+        chosen = pl.ds(0, 2 * rows_part * NBLK if part < 2 else 4 * rows_part)
+        return pltpu.make_async_remote_copy(
+            src_ref=far_made.at[part, chosen],
+            dst_ref=far_given.at[part, chosen],
+            send_sem=far_sem.at[0, part],
+            recv_sem=far_sem.at[1, part],
+            device_id={"tile": neighbour(LEFT)},
+            device_id_type=pl.DeviceIdType.MESH,
+        )
+
     def own_copy(half):
         return pltpu.make_async_copy(x_ref.at[half, 0], held.at[half, me], local_sem.at[half])
 
@@ -288,7 +308,7 @@
             transfer(block, half, SIBLING).start()
 
     def take_from_sibling(z_static, late):
-        for home in range(depth):
+        for home in range(depth if z_static else last):
             for row_of in range(ROWS):
                 if is_late(depth, z_static, (0, home, row_of)) != late:
                     continue
@@ -319,15 +339,15 @@
         stacked = jnp.concatenate(
             [jnp.concatenate(halves, axis=1), jnp.concatenate([halves[1], -halves[0]], axis=1)], axis=0
         )
-        lhs[2 * rows_part * block : 2 * rows_part * (block + 1), :] = stacked.astype(jnp.bfloat16)
-
-    def pair_product(first):
-        used = 2 * rows_part * (first + 2)
+        lhs[pl.ds(pl.multiple_of(block * 2 * rows_part, 2 * rows_part), 2 * rows_part), :] = stacked.astype(jnp.bfloat16)
+
+    def pair_product(first, begin=0, used=None):
+        used = 2 * rows_part * (first + 2) if used is None else used
         total = None
         for half in range(2):
-            columns = held[half, first : first + 2].reshape(2 * width, time)
+            columns = held[half, pl.ds(first, 2)].reshape(2 * width, time)
             product = lax.dot_general(
-                lhs[:used, half * time : (half + 1) * time],
+                lhs[pl.ds(begin, used), half * time : (half + 1) * time],
                 columns,
                 (((1,), (1,)), ((), ())),
                 preferred_element_type=jnp.float32,
@@ -335,12 +355,12 @@
             total = product if total is None else total + product
         return total * (1.0 / time)
 
-    def spread(first, total):
+    def spread(first, total, row_blocks=None, offset=0):
         for col_block in (first, first + 1):
             shift = (col_block - first) * width
-            for row_block in range(col_block + 1):
-                for part in range(2):
-                    top = (2 * row_block + part) * rows_part
+            for row_block in range(col_block + 1) if row_blocks is None else row_blocks:
+                for part in range(2 if row_block <= col_block else 0):
+                    top = (2 * (row_block - offset) + part) * rows_part
                     out_ref[part, 0, tile_number(row_block, col_block)] = total[top : top + rows_part, shift : shift + width]
 
     chip_blocks = ROWS * CORES
@@ -354,7 +374,29 @@
             total = pair_product(first)
             made[first // 2, : total.shape[0], :] = total
 
-    for block in range(NBLK - chip_blocks):
+    @pl.when(z == 1)
+    def _():
+        there = NBLK - chip_blocks + 2 * row
+        later = NBLK - chip_blocks + 2 * (1 - row)
+        everything = 2 * rows_part * NBLK
+        for block in range(NBLK - chip_blocks):
+            set_rows(block, me - chip_blocks)
+        for step in range(2):
+            set_rows(there + step, me - chip_blocks)
+        far_made[0] = pair_product(there, 0, everything)
+        far_handover(0).start()
+        take_in(1, True)
+        take_from_sibling(1, True)
+        for step in range(2):
+            set_rows(later + step, me - chip_blocks)
+        far_made[1] = pair_product(later, 0, everything)
+        begin = pl.multiple_of(later * 2 * rows_part, 4 * rows_part)
+        far_made[2, : 4 * rows_part] = pair_product(there, begin, 4 * rows_part)
+        far_handover(1).start()
+        far_handover(2).start()
+
+    middle = NBLK // 2
+    for block in range(middle):
         set_rows(block, me)
 
     @pl.when(z == last - 1)
@@ -366,7 +408,7 @@
         for first in handed:
             spread(first, pair_product(first))
 
-    for first in range(chip_blocks, NBLK - chip_blocks, 2):
+    for first in range(chip_blocks, middle, 2):
         spread(first, pair_product(first))
 
     @pl.when(z == 0)
@@ -374,10 +416,35 @@
         take_in(0, True)
         take_from_sibling(0, True)
 
-    for block in range(NBLK - chip_blocks, NBLK):
+    for block in range(middle, NBLK - chip_blocks):
         set_rows(block, me)
-    for first in range(NBLK - chip_blocks, NBLK, 2):
+    for first in range(middle, NBLK - chip_blocks, 2):
         spread(first, pair_product(first))
+
+    @pl.when(z > 0)
+    def _():
+        for block in range(NBLK - chip_blocks, NBLK):
+            set_rows(block, me)
+        for first in range(NBLK - chip_blocks, NBLK, 2):
+            spread(first, pair_product(first))
+
+    for row_static in range(ROWS):
+
+        @pl.when(jnp.logical_and(z == 0, row == row_static))
+        def _():
+            there = NBLK - chip_blocks + 2 * row_static
+            later = NBLK - chip_blocks + 2 * (1 - row_static)
+            far_handover(0).wait_recv()
+            if row_static == 0:
+                spread(there, far_given[0])
+            else:
+                spread(there, far_given[0], range(later))
+                spread(there, far_given[0], range(there, there + 2))
+            far_handover(1).wait_recv()
+            spread(later, far_given[1])
+            far_handover(2).wait_recv()
+            if row_static == 1:
+                spread(there, far_given[2], range(later, later + 2), later)
 
     @pl.when(z == last)
     def _():
@@ -405,6 +472,9 @@
                 transfer(block, half, SIBLING).wait_send()
             if z_static == last - 1:
                 handover().wait_send()
+            if z_static == 1:
+                for part in range(3):
+                    far_handover(part).wait_send()
             if z_static == last:
                 for home_row, half in thin_items:
                     transfer(index_of(0, home_row, core), half, SIBLING, chip).wait_send()
@@ -431,10 +501,13 @@
             pltpu.VMEM((2 * rows_part * NBLK, 2 * time), jnp.bfloat16),
             pltpu.VMEM((ROWS, 2 * rows_part * ROWS * CORES, 2 * width), jnp.float32),
             pltpu.VMEM((ROWS, 2 * rows_part * ROWS * CORES, 2 * width), jnp.float32),
+            pltpu.VMEM((3, 2 * rows_part * NBLK, 2 * width), jnp.float32),
+            pltpu.VMEM((3, 2 * rows_part * NBLK, 2 * width), jnp.float32),
             pltpu.SemaphoreType.DMA((2,)),
             pltpu.SemaphoreType.DMA((4, NBLK, 2)),
             pltpu.SemaphoreType.DMA((NBLK, 2)),
             pltpu.SemaphoreType.DMA((2,)),
+            pltpu.SemaphoreType.DMA((2, 3)),
         ],
         compiler_params=pltpu.CompilerParams(
             collective_id=0, has_side_effects=True, vmem_limit_bytes=24 * 2**20

time: 50.3 us -> 47.9 us (0.952)
  Pallas kernels: 49.1 us -> 46.7 us
    pallas_call x1, Pallas kernels: 48.1 us -> 45.7 us  [gathered(): pl.pallas_call(lambda *refs: correlate_kernel(depth, *refs), out_shape=ja...]
where the time goes in v3:
time: 47.9 us; the launch traced here: 47.8 us
  Pallas kernels  46.7 us (97%)
  local copies, waits for them, and re-layouts  1.04 us (2%)
    pallas_call x1, Pallas kernels, gathered(): pl.pallas_call(lambda *refs: correlate_kernel(depth, *refs), out_shape=ja...  45.7 us
    unnamed x2, local copies, waits for them, and re-layouts  1.04 us
    pallas_call x1, Pallas kernels, gathered(): pl.pallas_call(write_out, out_shape=jax.ShapeDtypeStruct(tiled.shape, til...  1 us

profile of v3, /device:TPU:1, one launch (start us, length us, event | category | flops | bytes accessed | tf_op | source)
XLA Modules:
  0.0 47.8 jit_solution(6755181039584600794)
XLA Ops:
  0.0 0.0 copy-start
  0.0 1.0 %copy-done = bf16[2,1,128,1024]{3,2,1,0:T(8,128)(2,1)S(1)} copy-done((bf16[2,1,128,1024]{3,2,1,0:T(8,128)(2,1)S(1)}, bf16[2,1,128,1024]{3,2,1,0:T(8,128)(2,1)}, u32[]{:S(2)}) %copy-start) | copy-done | bytes 524312
  1.0 45.7 %shard_map.17.tiled_ref = f32[2,1,136,8,128]{4,3,2,1,0:T(8,128)S(1)} custom-call(bf16[2,1,128,1024]{3,2,1,0:T(8,128)(2,1)S(1)} %copy-done), custom_call_target="tpu_custom_call" | custom-call | tf_op jit(solution)/shard_map/pallas_call | solution.py:494
  46.8 1.0 %shard_map.18 = f32[2,1,136,8,128]{4,3,2,1,0:T(8,128)} custom-call(f32[2,1,136,8,128]{4,3,2,1,0:T(8,128)S(1)} %shard_map.17.tiled_ref), custom_call_target="tpu_custom_call" | custom-call | tf_op jit(solution)/shard_map/pallas_call | solution.py:516
Async XLA Ops:
  0.0 1.0 %copy-start = (bf16[2,1,128,1024]{3,2,1,0:T(8,128)(2,1)S(1)}, bf16[2,1,128,1024]{3,2,1,0:T(8,128)(2,1)}, u32[]{:S(2)}) copy-start(bf16[2,1,128,1024]{3,2,1,0:T(8,128)(2,1)} %refs_0_.1) | copy-start | bytes 1572868

commit v4 on v3

--- a/solution.py
+++ b/solution.py
@@ -184,7 +184,7 @@
     return row_block * NBLK - row_block * (row_block - 1) // 2 + col_block - row_block
 
 
-def correlate_kernel(depth, x_ref, out_ref, held, lhs, made, given, far_made, far_given, local_sem, send_sem, recv_sem, made_sem, far_sem):
+def correlate_kernel(depth, x_ref, out_ref, held, lhs, made, given, far_made, far_given, side_made, side_given, local_sem, send_sem, recv_sem, made_sem, far_sem):
     me = lax.axis_index("tile")
     z = me // (ROWS * CORES)
     row = (me // CORES) % ROWS
@@ -238,11 +238,18 @@
             device_id_type=pl.DeviceIdType.MESH,
         )
 
-    def far_handover(part):
-        chosen = pl.ds(0, 2 * rows_part * NBLK if part < 2 else 4 * rows_part)
+    chip_blocks = ROWS * CORES
+
+    def far_handover(part, row_static):
+        late_base = NBLK - chip_blocks
+        blocks = {0: late_base + 2 + 2 * row_static, 1: late_base + 2 - 2 * row_static, 3: 2, 4: 2}
+        blocks[2] = blocks[1]
+        chosen = pl.ds(0, 2 * rows_part * blocks[part])
+        source, target = (far_made, far_given) if part in (0, 3, 4) else (side_made, side_given)
+        slot = {0: 0, 1: 0, 2: 1, 3: 1, 4: 2}[part]
         return pltpu.make_async_remote_copy(
-            src_ref=far_made.at[part, chosen],
-            dst_ref=far_given.at[part, chosen],
+            src_ref=source.at[slot, chosen],
+            dst_ref=target.at[slot, chosen],
             send_sem=far_sem.at[0, part],
             recv_sem=far_sem.at[1, part],
             device_id={"tile": neighbour(LEFT)},
@@ -341,11 +348,11 @@
         )
         lhs[pl.ds(pl.multiple_of(block * 2 * rows_part, 2 * rows_part), 2 * rows_part), :] = stacked.astype(jnp.bfloat16)
 
-    def pair_product(first, begin=0, used=None):
+    def pair_product(first, begin=0, used=None, count=2):
         used = 2 * rows_part * (first + 2) if used is None else used
         total = None
         for half in range(2):
-            columns = held[half, pl.ds(first, 2)].reshape(2 * width, time)
+            columns = held[half, pl.ds(first, count)].reshape(count * width, time)
             product = lax.dot_general(
                 lhs[pl.ds(begin, used), half * time : (half + 1) * time],
                 columns,
@@ -355,6 +362,12 @@
             total = product if total is None else total + product
         return total * (1.0 / time)
 
+    def spread_block(col_block, total, row_blocks):
+        for row_block in row_blocks:
+            for part in range(2):
+                top = (2 * row_block + part) * rows_part
+                out_ref[part, 0, tile_number(row_block, col_block)] = total[top : top + rows_part]
+
     def spread(first, total, row_blocks=None, offset=0):
         for col_block in (first, first + 1):
             shift = (col_block - first) * width
@@ -363,7 +376,6 @@
                     top = (2 * (row_block - offset) + part) * rows_part
                     out_ref[part, 0, tile_number(row_block, col_block)] = total[top : top + rows_part, shift : shift + width]
 
-    chip_blocks = ROWS * CORES
     handed = range(0, chip_blocks, 2)
 
     @pl.when(z == last - 1)
@@ -384,16 +396,38 @@
         for step in range(2):
             set_rows(there + step, me - chip_blocks)
         far_made[0] = pair_product(there, 0, everything)
-        far_handover(0).start()
+        for row_static in range(ROWS):
+
+            @pl.when(row == row_static)
+            def _():
+                far_handover(0, row_static).start()
+
         take_in(1, True)
+        begin = pl.multiple_of(later * 2 * rows_part, 4 * rows_part)
+        side_made[0] = pair_product(later + core, 0, everything - 4 * rows_part, 1)
+        for row_static in range(ROWS):
+
+            @pl.when(row == row_static)
+            def _():
+                far_handover(1, row_static).start()
+
         take_from_sibling(1, True)
+        side_made[1] = pair_product(later + 1 - core, 0, everything - 4 * rows_part, 1)
+        for row_static in range(ROWS):
+
+            @pl.when(row == row_static)
+            def _():
+                far_handover(2, row_static).start()
+
         for step in range(2):
             set_rows(later + step, me - chip_blocks)
-        far_made[1] = pair_product(later, 0, everything)
-        begin = pl.multiple_of(later * 2 * rows_part, 4 * rows_part)
-        far_made[2, : 4 * rows_part] = pair_product(there, begin, 4 * rows_part)
-        far_handover(1).start()
-        far_handover(2).start()
+        far_made[1, : 4 * rows_part] = pair_product(later, begin, 4 * rows_part)
+        far_handover(3, 0).start()
+
+        @pl.when(row == 1)
+        def _():
+            far_made[2, : 4 * rows_part] = pair_product(there, begin, 4 * rows_part)
+            far_handover(4, 1).start()
 
     middle = NBLK // 2
     for block in range(middle):
@@ -434,16 +468,21 @@
         def _():
             there = NBLK - chip_blocks + 2 * row_static
             later = NBLK - chip_blocks + 2 * (1 - row_static)
-            far_handover(0).wait_recv()
-            if row_static == 0:
-                spread(there, far_given[0])
-            else:
-                spread(there, far_given[0], range(later))
-                spread(there, far_given[0], range(there, there + 2))
-            far_handover(1).wait_recv()
-            spread(later, far_given[1])
-            far_handover(2).wait_recv()
+            far_handover(0, row_static).wait_recv()
+            spread(there, far_given[0], [block for block in range(there + 2) if block < min(there, later) or block >= there])
+            for part in (1, 2):
+                far_handover(part, row_static).wait_recv()
+                for core_static in range(CORES):
+
+                    @pl.when(core == core_static)
+                    def _():
+                        own_late = core_static if part == 1 else 1 - core_static
+                        spread_block(later + own_late, side_given[part - 1], range(later))
+
+            far_handover(3, 0).wait_recv()
+            spread(later, far_given[1], range(later, later + 2), later)
             if row_static == 1:
+                far_handover(4, 1).wait_recv()
                 spread(there, far_given[2], range(later, later + 2), later)
 
     @pl.when(z == last)
@@ -473,8 +512,13 @@
             if z_static == last - 1:
                 handover().wait_send()
             if z_static == 1:
-                for part in range(3):
-                    far_handover(part).wait_send()
+                for row_static in range(ROWS):
+
+                    @pl.when(row == row_static)
+                    def _():
+                        for part in range(4 + row_static):
+                            far_handover(part, row_static).wait_send()
+
             if z_static == last:
                 for home_row, half in thin_items:
                     transfer(index_of(0, home_row, core), half, SIBLING, chip).wait_send()
@@ -503,11 +547,13 @@
             pltpu.VMEM((ROWS, 2 * rows_part * ROWS * CORES, 2 * width), jnp.float32),
             pltpu.VMEM((3, 2 * rows_part * NBLK, 2 * width), jnp.float32),
             pltpu.VMEM((3, 2 * rows_part * NBLK, 2 * width), jnp.float32),
+            pltpu.VMEM((2, 2 * rows_part * (NBLK - 2), width), jnp.float32),
+            pltpu.VMEM((2, 2 * rows_part * (NBLK - 2), width), jnp.float32),
             pltpu.SemaphoreType.DMA((2,)),
             pltpu.SemaphoreType.DMA((4, NBLK, 2)),
             pltpu.SemaphoreType.DMA((NBLK, 2)),
             pltpu.SemaphoreType.DMA((2,)),
-            pltpu.SemaphoreType.DMA((2, 3)),
+            pltpu.SemaphoreType.DMA((2, 5)),
         ],
         compiler_params=pltpu.CompilerParams(
             collective_id=0, has_side_effects=True, vmem_limit_bytes=24 * 2**20

time: 47.9 us -> 47 us (0.981)
  the two profiles are of different devices: /device:TPU:1 before, /device:TPU:0 now
where the time goes in v4:
time: 47 us; the launch traced here: 46.8 us
  Pallas kernels  45.7 us (97%)
  local copies, waits for them, and re-layouts  1.04 us (2%)
    pallas_call x1, Pallas kernels, gathered(): pl.pallas_call(lambda *refs: correlate_kernel(depth, *refs), out_shape=ja...  44.7 us
    unnamed x2, local copies, waits for them, and re-layouts  1.04 us
    pallas_call x1, Pallas kernels, gathered(): pl.pallas_call(write_out, out_shape=jax.ShapeDtypeStruct(tiled.shape, til...  1 us

profile of v4, /device:TPU:0, one launch (start us, length us, event | category | flops | bytes accessed | tf_op | source)
XLA Modules:
  0.0 46.8 jit_solution(17502344343523894248)
XLA Ops:
  0.0 0.0 copy-start
  0.0 1.0 %copy-done = bf16[2,1,128,1024]{3,2,1,0:T(8,128)(2,1)S(1)} copy-done((bf16[2,1,128,1024]{3,2,1,0:T(8,128)(2,1)S(1)}, bf16[2,1,128,1024]{3,2,1,0:T(8,128)(2,1)}, u32[]{:S(2)}) %copy-start) | copy-done | bytes 524312
  1.0 44.7 %shard_map.17.tiled_ref = f32[2,1,136,8,128]{4,3,2,1,0:T(8,128)S(1)} custom-call(bf16[2,1,128,1024]{3,2,1,0:T(8,128)(2,1)S(1)} %copy-done), custom_call_target="tpu_custom_call" | custom-call | tf_op jit(solution)/shard_map/pallas_call | solution.py:538
  45.8 1.0 %shard_map.18 = f32[2,1,136,8,128]{4,3,2,1,0:T(8,128)} custom-call(f32[2,1,136,8,128]{4,3,2,1,0:T(8,128)S(1)} %shard_map.17.tiled_ref), custom_call_target="tpu_custom_call" | custom-call | tf_op jit(solution)/shard_map/pallas_call | solution.py:562
Async XLA Ops:
  0.0 1.0 %copy-start = (bf16[2,1,128,1024]{3,2,1,0:T(8,128)(2,1)S(1)}, bf16[2,1,128,1024]{3,2,1,0:T(8,128)(2,1)}, u32[]{:S(2)}) copy-start(bf16[2,1,128,1024]{3,2,1,0:T(8,128)(2,1)} %refs_0_.1) | copy-start | bytes 1572868

commit v5 on v4

--- a/solution.py
+++ b/solution.py
@@ -125,11 +125,11 @@
     high = last - 1 if home == 0 else last
     edges = [(z, 0, LEFT) for z in range(home, low, -1)] + [(z, 0, RIGHT) for z in range(home, high)]
     if home == 0:
-        reach = high if half == 1 else high - 1
+        reach = high if half == 0 else high - 1
         edges += [(z, 1, RIGHT) for z in range(home, reach)]
         crossings = [home] + list(range(reach + 1, high + 1))
     elif home == last:
-        reach = low if half == 1 else low + 1
+        reach = low if half == 0 else low + 1
         edges += [(z, 1, LEFT) for z in range(home, reach, -1)]
         crossings = [home] + list(range(low, reach))
     elif home == 1 and half == 1:
@@ -154,24 +154,26 @@
     link_free = {}
     pending = []
     order = 0
-    for half in range(2):
+    for along, half in ((True, 1), (False, 0), (True, 0), (False, 1)):
         for home in range(depth):
-            pending.append((0.0, order, home, half, home, 0))
+            pending.append((0.0, order, home, half, home, 0, along))
             order += 1
     events = {z: [] for z in range(depth)}
     while pending:
         pending.sort()
-        time, _, home, half, z, row = pending.pop(0)
+        time, _, home, half, z, row, along = pending.pop(0)
         ways = onward.get((home, half, z, row), [])
         if (z, row) != (home, 0):
             events[z].append((time, home, row, half, tuple(ways)))
         for way in ways:
+            if along is not None and along != (way != ACROSS):
+                continue
             for mirrored in (0, 1):
                 link_free.setdefault((z, way), 0.0)
             begin = max(time, link_free[(z, way)])
             link_free[(z, way)] = begin + 1.0
             nz, nrow = landing((z, row, way))
-            pending.append((begin + 1.1, order, home, half, nz, nrow))
+            pending.append((begin + 1.1, order, home, half, nz, nrow, None))
             order += 1
     return {z: sorted(found) for z, found in events.items()}
 
@@ -285,6 +287,7 @@
 
     for half in range(2):
         own_copy(half).wait()
+    for half in (1, 0):
 
         @pl.when(z > 0)
         def _():
@@ -294,7 +297,8 @@
         def _():
             transfer(me, half, RIGHT).start()
 
-        transfer(me, half, ACROSS).start()
+        transfer(me, 1 - half, ACROSS).start()
+    for half in range(2):
         transfer(me, half, SIBLING).start()
 
     plan = arrival_plan(depth)

time: 47 us -> 46.4 us (0.987)
  the two profiles are of different devices: /device:TPU:0 before, /device:TPU:1 now
where the time goes in v5:
time: 46.4 us; the launch traced here: 46.2 us
  Pallas kernels  45.1 us (97%)
  local copies, waits for them, and re-layouts  1.04 us (2%)
    pallas_call x1, Pallas kernels, gathered(): pl.pallas_call(lambda *refs: correlate_kernel(depth, *refs), out_shape=ja...  44.1 us
    unnamed x2, local copies, waits for them, and re-layouts  1.04 us
    pallas_call x1, Pallas kernels, gathered(): pl.pallas_call(write_out, out_shape=jax.ShapeDtypeStruct(tiled.shape, til...  1 us

profile of v5, /device:TPU:1, one launch (start us, length us, event | category | flops | bytes accessed | tf_op | source)
XLA Modules:
  0.0 46.2 jit_solution(15608662544428534099)
XLA Ops:
  0.0 0.0 copy-start
  0.0 1.0 %copy-done = bf16[2,1,128,1024]{3,2,1,0:T(8,128)(2,1)S(1)} copy-done((bf16[2,1,128,1024]{3,2,1,0:T(8,128)(2,1)S(1)}, bf16[2,1,128,1024]{3,2,1,0:T(8,128)(2,1)}, u32[]{:S(2)}) %copy-start) | copy-done | bytes 524312
  1.0 44.1 %shard_map.17.tiled_ref = f32[2,1,136,8,128]{4,3,2,1,0:T(8,128)S(1)} custom-call(bf16[2,1,128,1024]{3,2,1,0:T(8,128)(2,1)S(1)} %copy-done), custom_call_target="tpu_custom_call" | custom-call | tf_op jit(solution)/shard_map/pallas_call | solution.py:542
  45.2 1.0 %shard_map.18 = f32[2,1,136,8,128]{4,3,2,1,0:T(8,128)} custom-call(f32[2,1,136,8,128]{4,3,2,1,0:T(8,128)S(1)} %shard_map.17.tiled_ref), custom_call_target="tpu_custom_call" | custom-call | tf_op jit(solution)/shard_map/pallas_call | solution.py:566
Async XLA Ops:
  0.0 1.0 %copy-start = (bf16[2,1,128,1024]{3,2,1,0:T(8,128)(2,1)S(1)}, bf16[2,1,128,1024]{3,2,1,0:T(8,128)(2,1)}, u32[]{:S(2)}) copy-start(bf16[2,1,128,1024]{3,2,1,0:T(8,128)(2,1)} %refs_0_.1) | copy-start | bytes 1572868

commit v6 on v5

--- a/solution.py
+++ b/solution.py
@@ -449,6 +449,15 @@
     for first in range(chip_blocks, middle, 2):
         spread(first, pair_product(first))
 
+    for row_static in range(ROWS):
+
+        @pl.when(jnp.logical_and(z == 0, row == row_static))
+        def _():
+            there = NBLK - chip_blocks + 2 * row_static
+            later = NBLK - chip_blocks + 2 * (1 - row_static)
+            far_handover(0, row_static).wait_recv()
+            spread(there, far_given[0], [block for block in range(there + 2) if block < min(there, later) or block >= there])
+
     @pl.when(z == 0)
     def _():
         take_in(0, True)
@@ -472,8 +481,6 @@
         def _():
             there = NBLK - chip_blocks + 2 * row_static
             later = NBLK - chip_blocks + 2 * (1 - row_static)
-            far_handover(0, row_static).wait_recv()
-            spread(there, far_given[0], [block for block in range(there + 2) if block < min(there, later) or block >= there])
             for part in (1, 2):
                 far_handover(part, row_static).wait_recv()
                 for core_static in range(CORES):
@@ -562,7 +569,7 @@
         compiler_params=pltpu.CompilerParams(
             collective_id=0, has_side_effects=True, vmem_limit_bytes=24 * 2**20
         ),
-    )(voltages)
+    )(pltpu.with_memory_space_constraint(voltages, pltpu.HBM))
     return pl.pallas_call(
         write_out,
         out_shape=jax.ShapeDtypeStruct(tiled.shape, tiled.dtype),

time: 46.4 us -> 45.3 us (0.976)
  local copies, waits for them, and re-layouts: 1.04 us -> 0 us
    unnamed x2 -> x0, local copies, waits for them, and re-layouts: 1.04 us -> none
where the time goes in v6:
time: 45.3 us; the launch traced here: 45.1 us
  Pallas kernels  45.1 us (100%)
    pallas_call x1, Pallas kernels, gathered(): pl.pallas_call(lambda *refs: correlate_kernel(depth, *refs), out_shape=ja...  44.1 us
    pallas_call x1, Pallas kernels, gathered(): pl.pallas_call(write_out, out_shape=jax.ShapeDtypeStruct(tiled.shape, til...  1 us

profile of v6, /device:TPU:1, one launch (start us, length us, event | category | flops | bytes accessed | tf_op | source)
XLA Modules:
  0.0 45.1 jit_solution(8818752073071918449)
XLA Ops:
  0.0 44.1 %shard_map.17.tiled_ref = f32[2,1,136,8,128]{4,3,2,1,0:T(8,128)S(1)} custom-call(bf16[2,1,128,1024]{3,2,1,0:T(8,128)(2,1)} %refs_0_.1), custom_call_target="tpu_custom_call" | custom-call | tf_op jit(solution)/shard_map/pallas_call | solution.py:549
  44.1 1.0 %shard_map.18 = f32[2,1,136,8,128]{4,3,2,1,0:T(8,128)} custom-call(f32[2,1,136,8,128]{4,3,2,1,0:T(8,128)S(1)} %shard_map.17.tiled_ref), custom_call_target="tpu_custom_call" | custom-call | tf_op jit(solution)/shard_map/pallas_call | solution.py:573
